TPU v7x, 128 devices: a whole 4x4x4 slice. The times are simulated.
128 devices in a mesh: node: 8 (over z, core), local: 16 (over y, x).
Axes of the slice: x: 4, y: 4, z: 4, core: 2. Of those that a mesh axis runs over, the one named last changes fastest.
Arguments:
- tokens: bfloat16 [2048, 7168], P(('node', 'local')), may hold values from -6 to 6
- grad_out: bfloat16 [2048, 7168], P(('node', 'local')), may hold values from -6 to 6
- gates: bfloat16 [2048, 3], P(('node', 'local')), may hold values from 0.19921875 to 1
- expert_ids: int32 [2048, 3], P(('node', 'local')), may hold values from 0 to 15, as said below
- w_gate: bfloat16 [8, 7168, 2048], P('node', None, 'local'), may hold values from -0.0625 to 0.0625
- w_up: bfloat16 [8, 7168, 2048], P('node', None, 'local'), may hold values from -0.0625 to 0.0625
- w_down: bfloat16 [8, 7168, 2048], P('node', None, 'local'), may hold values from -0.1875 to 0.1875
- s_gate: bfloat16 [7168, 2048], P(None, 'local'), may hold values from -0.0625 to 0.0625
- s_up: bfloat16 [7168, 2048], P(None, 'local'), may hold values from -0.0625 to 0.0625
- s_down: bfloat16 [7168, 2048], P(None, 'local'), may hold values from -0.125 to 0.125
Outputs:
- dx: bfloat16 [2048, 7168], P(('node', 'local'))
- dgates: float32 [2048, 3], P(('node', 'local'))
- d_w_gate: bfloat16 [8, 7168, 2048], P('node', None, 'local')
- d_w_up: bfloat16 [8, 7168, 2048], P('node', None, 'local')
- d_w_down: bfloat16 [8, 7168, 2048], P('node', None, 'local')
- d_s_gate: bfloat16 [7168, 2048], P('node', 'local')
- d_s_up: bfloat16 [7168, 2048], P('node', 'local')
- d_s_down: bfloat16 [7168, 2048], P('node', 'local')
Inputs may be any that keep to these rules, and one draw needn't show every extreme that they name: `expert_ids`: each token names both experts of one node and one expert of a second node. Of the tokens of one device exactly 4 name experts of each node and at most 4 name any one expert; for every node one of its experts is named by exactly 4 tokens of every device.
All inputs are finite; a program needn't handle non-finite values.
Results may differ from a plain program's by a relative error of at most 0.014.
Values may be sent and summed in bfloat16 or wider, within the bound.
No kernel may reach another device: no remote copies, remote signals or barrier semaphores. Data moves between devices by JAX's collectives and lax.ppermute only.
A program may use at most 192 MiB of HBM per device.

v0:
```python
import jax
import jax.numpy as jnp
from jax import lax
from jax.sharding import PartitionSpec as P

E_NODE = 2
precise = lax.Precision.HIGHEST


def split_up(value, dim, devices):
    before, after = (value.shape[:dim], value.shape[dim + 1 :])
    return jnp.moveaxis(value.reshape(*before, devices, -1, *after), dim, 0)


def summed_on_arrival(value, axis, dim):
    tiles = split_up(value, dim, lax.axis_size(axis))
    arrived = lax.all_to_all(tiles, axis, split_axis=0, concat_axis=0, tiled=True)
    return arrived.astype(jnp.float32).sum(axis=0)


def in_one_piece(arrays, axis, split_dim, concat_dim, along):
    columns = [a.reshape(*a.shape[:along], -1) for a in arrays]
    both = jnp.concatenate(columns, axis=along)
    out, at, gathered = (
        lax.all_to_all(both, axis, split_axis=split_dim, concat_axis=concat_dim, tiled=True),
        0,
        [],
    )
    for a, column in zip(arrays, columns):
        piece = out[..., at : at + column.shape[along]]
        gathered.append(piece.reshape(*piece.shape[:along], *a.shape[along:]))
        at += column.shape[along]
    return tuple(gathered)


def silu_parts(pre_gate):
    sig = jax.nn.sigmoid(pre_gate)
    return (pre_gate * sig, sig * (1.0 + pre_gate * (1.0 - sig)))


def contract_first(left, right):
    return lax.dot_general(
        left, right, (((0,), (0,)), ((), ())), preferred_element_type=jnp.float32
    )


def contract_last(left, right):
    return lax.dot_general(
        left, right, (((1,), (1,)), ((), ())), preferred_element_type=jnp.float32
    )


def ffn_backward(rows_in, rows_grad, weight, gate_w, up_w, down_w):
    pre_gate = jnp.dot(rows_in, gate_w, preferred_element_type=jnp.float32)
    pre_up = jnp.dot(rows_in, up_w, preferred_element_type=jnp.float32)
    activ, slope = silu_parts(pre_gate)
    hidden = activ * pre_up
    upstream = jnp.dot(rows_grad, down_w, preferred_element_type=jnp.float32)
    scaled = weight * upstream
    grad_up = (scaled * activ).astype(jnp.bfloat16)
    grad_gate = (scaled * pre_up * slope).astype(jnp.bfloat16)
    weighted = (weight * hidden).astype(jnp.bfloat16)
    return (grad_gate, grad_up, weighted, hidden * upstream)


def expert_work(rows_in, rows_grad, weight, gate_w, up_w, down_w):
    grad_gate, grad_up, weighted, product = ffn_backward(
        rows_in, rows_grad, weight, gate_w, up_w, down_w
    )
    partial_value = (contract_last(grad_gate, gate_w) + contract_last(grad_up, up_w)).astype(
        jnp.bfloat16
    )
    score = jnp.sum(product, axis=1).astype(jnp.bfloat16)
    grads = (
        contract_first(rows_in, grad_gate),
        contract_first(rows_in, grad_up),
        contract_first(rows_grad, weighted),
    )
    return (partial_value, score, grads)


def shared_part(tokens, grad_out, s_gate, s_up, s_down):
    rows_in, rows_grad = (
        lax.all_gather(tokens, "local", axis=0, tiled=True),
        lax.all_gather(grad_out, "local", axis=0, tiled=True),
    )
    unit_weight = jnp.ones((rows_in.shape[0], 1), jnp.float32)
    grad_gate, grad_up, weighted, product = ffn_backward(
        rows_in, rows_grad, unit_weight, s_gate, s_up, s_down
    )
    dx_shared = summed_on_arrival(
        (contract_last(grad_gate, s_gate) + contract_last(grad_up, s_up)).astype(jnp.bfloat16),
        "local",
        0,
    )
    units = s_gate.shape[1]
    shares = lax.psum_scatter(
        jnp.concatenate(
            [
                contract_first(rows_in, grad_gate),
                contract_first(rows_in, grad_up),
                contract_first(rows_grad, weighted),
            ],
            axis=1,
        ).astype(jnp.bfloat16),
        "node",
        scatter_dimension=0,
        tiled=True,
    ).astype(jnp.float32)
    shared_grads = (
        shares[:, :units].astype(jnp.bfloat16),
        shares[:, units : 2 * units].astype(jnp.bfloat16),
        shares[:, 2 * units :].astype(jnp.bfloat16),
    )
    return (dx_shared, shared_grads)


def routed_part(tokens, grad_out, gates, expert_ids, gate_w, up_w, down_w):
    tokens_here = tokens.shape[0]
    width = tokens.shape[1]
    node_count = lax.axis_size("node")
    local_count = lax.axis_size("local")
    group_size = local_count // E_NODE
    capacity = 2 * tokens_here // node_count
    expert_count = E_NODE * node_count
    slots = jnp.arange(capacity, dtype=jnp.int32)
    chosen = expert_ids[:, :, None] == jnp.arange(expert_count, dtype=jnp.int32)[None, None, :]
    member = jnp.any(chosen, axis=1)
    weight = jnp.sum(jnp.where(chosen, gates.astype(jnp.float32)[:, :, None], 0.0), axis=1)
    ranking = jnp.cumsum(member.astype(jnp.int32), axis=0) - 1
    slot_pick = member[:, :, None] & (ranking[:, :, None] == slots[None, None, :])
    pick_float = slot_pick.astype(jnp.float32)
    slot_gate = jnp.einsum("tes,te->es", pick_float, weight, precision=precise)
    pick_rows = slot_pick.astype(jnp.bfloat16)
    send_in = jnp.einsum(
        "tes,td->esd", pick_rows, tokens, preferred_element_type=jnp.float32
    ).astype(jnp.bfloat16)
    send_grad = jnp.einsum(
        "tes,td->esd", pick_rows, grad_out, preferred_element_type=jnp.float32
    ).astype(jnp.bfloat16)

    def spread(values):
        shaped = values.reshape((node_count, E_NODE, 1) + values.shape[1:])
        wide = jnp.broadcast_to(shaped, (node_count, E_NODE, group_size) + values.shape[1:])
        return wide.reshape((node_count * local_count,) + values.shape[1:])

    got_in, got_grad, got_gate = in_one_piece(
        (spread(send_in), spread(send_grad), spread(slot_gate.astype(jnp.bfloat16))),
        ("node", "local"),
        0,
        0,
        2,
    )
    partial_value, score, grads = expert_work(
        got_in.reshape(-1, width),
        got_grad.reshape(-1, width),
        got_gate.reshape(-1, 1).astype(jnp.float32),
        gate_w,
        up_w,
        down_w,
    )
    back_dx, back_score = (
        lax.all_to_all(
            partial_value.reshape(got_in.shape),
            ("node", "local"),
            split_axis=0,
            concat_axis=0,
            tiled=True,
        ),
        lax.all_to_all(
            score.reshape(got_gate.shape),
            ("node", "local"),
            split_axis=0,
            concat_axis=0,
            tiled=True,
        ),
    )
    slot_dx = jnp.sum(
        back_dx.reshape(node_count, E_NODE, group_size, capacity, width).astype(jnp.float32), axis=2
    ).reshape(expert_count, capacity, width)
    slot_score = jnp.sum(
        back_score.reshape(node_count, E_NODE, group_size, capacity).astype(jnp.float32), axis=2
    ).reshape(expert_count, capacity)
    dx_routed = jnp.einsum("tes,esd->td", pick_float, slot_dx, precision=precise)
    token_score = jnp.einsum("tes,es->te", pick_float, slot_score, precision=precise)
    dgates = jnp.sum(jnp.where(chosen, token_score[:, None, :], 0.0), axis=2)
    return (dx_routed, dgates, grads)


def local(tokens, grad_out, gates, expert_ids, w_gate, w_up, w_down, s_gate, s_up, s_down):
    dx_routed, dgates, grads = routed_part(
        tokens, grad_out, gates, expert_ids, w_gate[0], w_up[0], w_down[0]
    )
    dx_shared, shared_grads = shared_part(tokens, grad_out, s_gate, s_up, s_down)
    dx = (dx_routed + dx_shared).astype(jnp.bfloat16)
    expert_grads = tuple((grad.astype(jnp.bfloat16)[None] for grad in grads))
    return (
        dx,
        dgates,
        expert_grads[0],
        expert_grads[1],
        expert_grads[2],
        shared_grads[0],
        shared_grads[1],
        shared_grads[2],
    )


def solution(mesh):
    placed = (
        P(("node", "local"), None),
        P(("node", "local"), None),
        P(("node", "local"), None),
        P(("node", "local"), None),
        P("node", None, "local"),
        P("node", None, "local"),
        P("node", None, "local"),
        P(None, "local"),
        P(None, "local"),
        P(None, "local"),
    )
    return jax.shard_map(
        local,
        mesh=mesh,
        in_specs=placed,
        out_specs=(
            P(("node", "local"), None),
            P(("node", "local"), None),
            P("node", None, "local"),
            P("node", None, "local"),
            P("node", None, "local"),
            P("node", "local"),
            P("node", "local"),
            P("node", "local"),
        ),
        check_vma=False,
    )
```

profile of v0, /device:TPU:11, one launch (start us, length us, event | category | flops | bytes accessed | tf_op | source)
XLA Modules:
  0.0 510.7 jit_solution(10965011893710607387)
XLA Ops:
  7.9 0.8 fusion.31
  8.7 0.7 convert_element_type.108
  9.4 0.8 select_reduce_fusion.3
  10.9 1.4 convolution_convert_fusion.6
  12.2 0.7 copy.89
  13.0 1.4 convolution_convert_fusion.7
  14.3 0.7 copy.88
  15.1 5.2 %broadcast_in_dim.60 = bf16[8,2,8,4,7168]{4,3,2,1,0:T(4,128)(2,1)} broadcast(bf16[8,2,4,7168]{3,2,1,0:T(4,128)(2,1)S(1)} %bitcast.98), dimensions={0,1,3,4} | broadcast | bytes 8257536 | tf_op jit(solution)/shard_map/broadcast_in_dim | solution.py:144
  20.3 5.2 %broadcast_in_dim.62 = bf16[8,2,8,4,7168]{4,3,2,1,0:T(4,128)(2,1)} broadcast(bf16[8,2,4,7168]{3,2,1,0:T(4,128)(2,1)S(1)} %bitcast.97), dimensions={0,1,3,4} | broadcast | bytes 8257536 | tf_op jit(solution)/shard_map/broadcast_in_dim | solution.py:144
  25.5 11.0 %pad_maximum_fusion = bf16[128,4,14337]{2,1,0:T(4,128)(2,1)} fusion(bf16[128,4,1]{2,1,0:T(4,128)(2,1)S(1)} %copy.67, bf16[128,4,7168]{2,1,0:T(4,128)(2,1)} %bitcast.94, bf16[128,4,7168]{2,1,0:T(4,128)(2,1)} %bitcast.93), kind=kLoop, calls=%fused_computation | loop fusion | flops 44043264 | bytes 29362176 | tf_op jit(solution)/shard_map/concatenate | solution.py:23
  36.5 11.2 %all-to-all-start = ((bf16[128,4,14337]{2,1,0:T(4,128)(2,1)}), bf16[128,4,14337]{2,1,0:T(4,128)(2,1)}, u32[]{:S(2)}, u32[]{:S(2)}) async-start(bf16[128,4,14337]{2,1,0:T(4,128)(2,1)} %pad_maximum_fusion), calls=%async_computation | async-start | bytes 29622272 | tf_op jit(solution)/shard_map/all_to_all | solution.py:25
  47.7 0.7 all-gather.3.cloned.1.call-update
  48.9 75.6 %all-gather.5.cloned.1.call-done = bf16[256,7168]{1,0:T(8,128)(2,1)} async-done(((bf16[16,7168]{1,0:T(8,128)(2,1)}), bf16[256,7168]{1,0:T(8,128)(2,1)}) %all-gather.5.cloned.1.call-update) | async-done | bytes 3670032 | tf_op jit(solution)/shard_map/all_gather | solution.py:84
  124.6 3.9 fusion.44
  128.8 1.2 fusion.43
  130.0 120.8 %all-gather.3.cloned.1.call-done = bf16[256,7168]{1,0:T(8,128)(2,1)} async-done(((bf16[16,7168]{1,0:T(8,128)(2,1)}), bf16[256,7168]{1,0:T(8,128)(2,1)}) %all-gather.3.cloned.1.call-update) | async-done | bytes 3670032 | tf_op jit(solution)/shard_map/all_gather | solution.py:85
  250.8 3.9 multiply_convert_fusion.5
  255.3 0.7 fusion.4
  256.0 1.3 copy-done.8
  257.4 0.7 fusion.6
  258.1 3.1 pad_maximum_fusion.1
  261.2 8.3 %copy.90 = bf16[7168,384]{1,0:T(8,128)(2,1)} copy(bf16[7168,384]{0,1:T(8,128)(2,1)} %pad_maximum_fusion.1) | data formatting | bytes 11010048
  269.5 2.7 fusion.45
  272.3 3.0 fusion
  275.2 11.3 %all-to-all-done = bf16[128,4,14337]{2,1,0:T(4,128)(2,1)} async-done(((bf16[128,4,14337]{2,1,0:T(4,128)(2,1)}), bf16[128,4,14337]{2,1,0:T(4,128)(2,1)}, u32[]{:S(2)}, u32[]{:S(2)}) %all-to-all-start) | async-done | bytes 14681120 | tf_op jit(solution)/shard_map/all_to_all | solution.py:25
  286.5 8.8 %all-to-all-start.2 = ((bf16[16,16,7168]{2,1,0:T(8,128)(2,1)}), bf16[16,16,7168]{2,1,0:T(8,128)(2,1)}, u32[]{:S(2)}, u32[]{:S(2)}) async-start(bf16[16,16,7168]{2,1,0:T(8,128)(2,1)} %bitcast.95), calls=%async_computation.2 | async-start | bytes 7340032 | tf_op jit(solution)/shard_map/all_to_all | solution.py:17
  295.3 15.1 %fusion.41 = (bf16[128,4,7168]{2,1,0:T(4,128)(2,1)}, bf16[128,4,7168]{2,1,0:T(4,128)(2,1)}) fusion(bf16[128,4,14337]{2,1,0:T(4,128)(2,1)} %all-to-all-done), kind=kLoop, calls=%fused_computation.68 | loop fusion | bytes 29360128 | tf_op jit(solution)/shard_map/slice | solution.py:30
  310.4 1.1 convert_reduce_fusion.2
  311.7 12.2 %reshape.92 = bf16[512,7168]{1,0:T(8,128)(2,1)} reshape(bf16[128,4,7168]{2,1,0:T(4,128)(2,1)} %get-tuple-element.48) | data formatting | bytes 14680064 | tf_op jit(solution)/shard_map/reshape | solution.py:156
  323.8 12.1 %reshape.93 = bf16[512,7168]{1,0:T(8,128)(2,1)} reshape(bf16[128,4,7168]{2,1,0:T(4,128)(2,1)} %get-tuple-element.49) | data formatting | bytes 14680064 | tf_op jit(solution)/shard_map/reshape | solution.py:155
  336.0 5.8 %fusion.11 = f32[512,128]{0,1:T(8,128)S(1)} fusion(bf16[512,7168]{1,0:T(8,128)(2,1)} %reshape.93, bf16[1,7168,128]{2,1,0:T(8,128)(2,1)S(1)} %copy-done), kind=kOutput, calls=%fused_computation.26 | convolution fusion | flops 939524096 | bytes 9437184 | tf_op jit(solution)/shard_map/dot_general | solution.py:54
  341.8 2.5 fusion.14
  345.4 2.6 multiply_reduce_fusion
  348.0 0.8 convert_element_type.134
  348.7 7.3 %fusion.9 = f32[512,7168]{1,0:T(8,128)} fusion(bf16[512,128]{0,1:T(8,128)(2,1)S(1)} %get-tuple-element.51, bf16[1,7168,128]{2,1,0:T(8,128)(2,1)S(1)} %copy-done), kind=kOutput, calls=%fused_computation.24 | convolution fusion | flops 939524096 | bytes 16646144 | tf_op jit(solution)/shard_map/dot_general | solution.py:48
  356.0 15.4 %all-to-all-start.3 = ((bf16[128,1,4]{2,1,0:T(2,128)(2,1)}), bf16[128,1,4]{2,1,0:T(2,128)(2,1)S(1)}, u32[]{:S(2)}, u32[]{:S(2)}) async-start(bf16[128,1,4]{2,1,0:T(2,128)(2,1)} %convert_element_type.134), calls=%async_computation.3 | async-start | bytes 131072 | tf_op jit(solution)/shard_map/all_to_all | solution.py:170
  371.5 10.7 %add_convert_fusion = bf16[512,7168]{1,0:T(8,128)(2,1)} fusion(f32[512,7168]{1,0:T(8,128)} %fusion.9, bf16[512,128]{0,1:T(8,128)(2,1)S(1)} %get-tuple-element.55, bf16[1,7168,128]{2,1,0:T(8,128)(2,1)} %param.15), kind=kOutput, calls=%fused_computation.2 | convolution fusion | flops 946864128 | bytes 23986176 | tf_op jit(solution)/shard_map/dot_general | solution.py:48
  382.2 12.7 %reshape.94 = bf16[128,4,7168]{2,1,0:T(4,128)(2,1)} reshape(bf16[512,7168]{1,0:T(8,128)(2,1)} %add_convert_fusion) | data formatting | bytes 14680064 | tf_op jit(solution)/shard_map/reshape | solution.py:164
  394.9 10.4 %all-to-all-start.1 = ((bf16[128,4,7168]{2,1,0:T(4,128)(2,1)}), bf16[128,4,7168]{2,1,0:T(4,128)(2,1)}, u32[]{:S(2)}, u32[]{:S(2)}) async-start(bf16[128,4,7168]{2,1,0:T(4,128)(2,1)} %reshape.94), calls=%async_computation.1 | async-start | bytes 14680064 | tf_op jit(solution)/shard_map/all_to_all | solution.py:163
  405.3 2.7 convert_reduce_fusion.1
  408.0 6.6 %fusion.1 = bf16[1,7168,128]{2,1,0:T(8,128)(2,1)} fusion(bf16[512,7168]{1,0:T(8,128)(2,1)} %reshape.93, bf16[512,128]{0,1:T(8,128)(2,1)S(1)} %get-tuple-element.51), kind=kOutput, calls=%fused_computation.11 | convolution fusion | flops 940441600 | bytes 9306112 | tf_op jit(solution)/shard_map/dot_general | solution.py:42
  414.7 3.4 fusion.2
  418.0 3.4 fusion.3
  421.7 0.7 select_reduce_fusion.2
  422.4 2.0 fusion.42
  424.4 70.0 %all-to-all-done.1 = bf16[128,4,7168]{2,1,0:T(4,128)(2,1)} async-done(((bf16[128,4,7168]{2,1,0:T(4,128)(2,1)}), bf16[128,4,7168]{2,1,0:T(4,128)(2,1)}, u32[]{:S(2)}, u32[]{:S(2)}) %all-to-all-start.1) | async-done | bytes 7340064 | tf_op jit(solution)/shard_map/all_to_all | solution.py:163
  494.4 6.8 %convert_reduce_fusion = f32[8,2,4,7168]{3,2,1,0:T(4,128)S(1)} fusion(bf16[128,4,7168]{2,1,0:T(4,128)(2,1)} %all-to-all-done.1), kind=kLoop, calls=%fused_computation.1 | loop fusion | flops 6881280 | bytes 9175040 | tf_op jit(solution)/shard_map/reduce_sum | solution.py:178
  501.2 2.7 fusion.8
  (54 shorter events, 4.4 us)
Async XLA Ops:
  7.2 328.8 %copy-start = (bf16[1,7168,128]{2,1,0:T(8,128)(2,1)S(1)}, bf16[1,7168,128]{2,1,0:T(8,128)(2,1)}, u32[]{:S(2)}) copy-start(bf16[1,7168,128]{2,1,0:T(8,128)(2,1)} %param.14) | copy-start | bytes 5505028
  7.2 117.4 %all-gather.5.cloned.1.call-start = ((), (), s32[]{:S(2)}) async-start(), calls=%async_computation.6 | async-start | bytes 3899392 | tf_op jit(solution)/shard_map/all_gather | solution.py:84
  36.5 250.1 %all-to-all-start = ((bf16[128,4,14337]{2,1,0:T(4,128)(2,1)}), bf16[128,4,14337]{2,1,0:T(4,128)(2,1)}, u32[]{:S(2)}, u32[]{:S(2)}) async-start(bf16[128,4,14337]{2,1,0:T(4,128)(2,1)} %pad_maximum_fusion), calls=%async_computation | async-start | bytes 29622272 | tf_op jit(solution)/shard_map/all_to_all | solution.py:25
  47.7 203.1 %all-gather.3.cloned.1.call-start = ((), (), s32[]{:S(2)}) async-start(), calls=%async_computation.5 | async-start | bytes 3899392 | tf_op jit(solution)/shard_map/all_gather | solution.py:85
  48.4 374.0 %reduce-scatter.4.cloned.1.call-start = ((), (), s32[]{:S(2)}) async-start(), calls=%async_computation.7 | async-start | bytes 6193152
  124.6 3.9 copy-start.3
  124.6 4.3 copy-start.6
  250.8 3.9 copy-start.4
  255.3 2.0 copy-start.8
  269.5 2.8 copy-start.7
  286.5 69.5 %all-to-all-start.2 = ((bf16[16,16,7168]{2,1,0:T(8,128)(2,1)}), bf16[16,16,7168]{2,1,0:T(8,128)(2,1)}, u32[]{:S(2)}, u32[]{:S(2)}) async-start(bf16[16,16,7168]{2,1,0:T(8,128)(2,1)} %bitcast.95), calls=%async_computation.2 | async-start | bytes 7340032 | tf_op jit(solution)/shard_map/all_to_all | solution.py:17
  336.0 5.8 %copy-start.1 = (bf16[512,7168]{1,0:T(8,128)(2,1)S(1)}, bf16[512,7168]{1,0:T(8,128)(2,1)}, u32[]{:S(2)}) copy-start(bf16[512,7168]{1,0:T(8,128)(2,1)} %reshape.93) | copy-start | bytes 22020100
  336.0 5.8 %copy-start.5 = (bf16[1,7168,128]{2,1,0:T(8,128)(2,1)S(1)}, bf16[1,7168,128]{2,1,0:T(8,128)(2,1)}, u32[]{:S(2)}) copy-start(bf16[1,7168,128]{2,1,0:T(8,128)(2,1)} %param.15) | copy-start | bytes 5505028
  341.8 3.1 copy-start.2
  341.8 3.6 copy-start.9
  356.0 38.8 %all-to-all-start.3 = ((bf16[128,1,4]{2,1,0:T(2,128)(2,1)}), bf16[128,1,4]{2,1,0:T(2,128)(2,1)S(1)}, u32[]{:S(2)}, u32[]{:S(2)}) async-start(bf16[128,1,4]{2,1,0:T(2,128)(2,1)} %convert_element_type.134), calls=%async_computation.3 | async-start | bytes 131072 | tf_op jit(solution)/shard_map/all_to_all | solution.py:170
  394.9 99.5 %all-to-all-start.1 = ((bf16[128,4,7168]{2,1,0:T(4,128)(2,1)}), bf16[128,4,7168]{2,1,0:T(4,128)(2,1)}, u32[]{:S(2)}, u32[]{:S(2)}) async-start(bf16[128,4,7168]{2,1,0:T(4,128)(2,1)} %reshape.94), calls=%async_computation.1 | async-start | bytes 14680064 | tf_op jit(solution)/shard_map/all_to_all | solution.py:163
  405.3 9.4 %slice-start = ((s8[7340032]{0:T(1024)(128)(4,1)}), s8[4194304]{0:T(1024)(128)(4,1)S(1)}, s32[]{:S(2)}) async-start(s8[7340032]{0:T(1024)(128)(4,1)} %bitcast.89), calls=%async_computation.8 | async-start | bytes 8388608
  408.0 6.6 %slice-start.1 = ((s8[7340032]{0:T(1024)(128)(4,1)}), s8[3145728]{0:T(1024)(128)(4,1)S(1)}, s32[]{:S(2)}) async-start(s8[7340032]{0:T(1024)(128)(4,1)} %bitcast.89), calls=%async_computation.9 | async-start | bytes 6291456
  408.0 10.0 %slice-start.2 = ((s8[7340032]{0:T(1024)(128)(4,1)}), s8[4194304]{0:T(1024)(128)(4,1)S(1)}, s32[]{:S(2)}) async-start(s8[7340032]{0:T(1024)(128)(4,1)} %bitcast.91), calls=%async_computation.10 | async-start | bytes 8388608
  414.7 3.4 slice-start.3
  418.0 3.6 copy-start.10
Sparse Core Ops, SparseCore 0:
  10.1 114.4 all-gather.4
  126.7 124.0 all-gather.2
  269.6 58.3 reduce-scatter.3
where the time goes:
time: 518 us; the launch traced here: 511 us
  waiting for transfers between devices  279 us (54%)
  local copies, waits for them, and re-layouts  78.7 us (15%)
  matrix products  64.5 us (12%)
  starting transfers between devices  46.4 us (9%)
  other arithmetic  27.8 us (5%)
  between operations  14.3 us (3%)
    all_gather x1, waiting for transfers between devices, shared_part(): lax.all_gather(grad_out, 'local', axis=0, tiled=True)  121 us
    all_gather x1, waiting for transfers between devices, shared_part(): lax.all_gather(tokens, 'local', axis=0, tiled=True)  75.6 us
    all_to_all x1, waiting for transfers between devices, routed_part(): lax.all_to_all(partial_value.reshape(got_in.shape), ('node', 'local'), sp...  70 us
    dot_general x4, matrix products, contract_last(): lax.dot_general(left, right, (((1,), (1,)), ((), ())), preferred_element_...  23.7 us
    dot_general x6, matrix products, contract_first(): lax.dot_general(left, right, (((0,), (0,)), ((), ())), preferred_element_...  15.5 us
    all_to_all x1, starting transfers between devices, routed_part(): lax.all_to_all(score.reshape(got_gate.shape), ('node', 'local'), split_ax...  15.4 us
    slice x1, local copies, waits for them, and re-layouts, in_one_piece(): piece = out[..., at:at + column.shape[along]]  15.1 us
    reshape x1, local copies, waits for them, and re-layouts, routed_part(): partial_value.reshape(got_in.shape)  12.7 us
  transfers between devices with their start and end apart: 7, of which 4 were waited for; matrix products, arithmetic and copies ran while one was open for 31% of the time, Pallas kernels for 0%

commit v1 on v0

--- a/solution.py
+++ b/solution.py
@@ -5,6 +5,28 @@
 
 E_NODE = 2
 precise = lax.Precision.HIGHEST
+
+
+def in_order(parts, dim):
+    lengths = list(parts.shape[1:])
+    lengths[dim] *= parts.shape[0]
+    return jnp.moveaxis(parts, 0, dim).reshape(lengths)
+
+
+def gather_around(x, axis, dim):
+    size = lax.axis_size(axis)
+    pairs = [(i, (i + 1) % size) for i in range(size)]
+    back = [(b, a) for a, b in pairs]
+    lower, upper = ([], [])
+    for step in range(size - 1):
+        if step % 2 == 0:
+            lower.append(lax.ppermute(lower[-1] if lower else x, axis, pairs))
+        else:
+            upper.append(lax.ppermute(upper[-1] if upper else x, axis, back))
+    parts = jnp.stack([*lower[::-1], x, *upper])
+    shift = lax.axis_index(axis) - len(lower)
+    parts = parts[(jnp.arange(size) - shift) % size]
+    return in_order(parts, dim)
 
 
 def split_up(value, dim, devices):
@@ -81,7 +103,7 @@
 
 def shared_part(tokens, grad_out, s_gate, s_up, s_down):
     rows_in, rows_grad = (
-        lax.all_gather(tokens, "local", axis=0, tiled=True),
+        gather_around(tokens, "local", 0),
         lax.all_gather(grad_out, "local", axis=0, tiled=True),
     )
     unit_weight = jnp.ones((rows_in.shape[0], 1), jnp.float32)

time: 518 us -> 591 us (1.14)
  starting transfers between devices: 46.4 us -> 105 us
  local copies, waits for them, and re-layouts: 78.7 us -> 101 us
  waiting for transfers between devices: 279 us -> 270 us
    ppermute x0 -> x15, waiting for transfers between devices: none -> 200 us  [the longest x7 178 us: gather_around(): upper.append(lax.ppermute(upper[-1] if upper else x, axis, back))]
    all_gather x1, waiting for transfers between devices: 121 us -> 0.02 us  [shared_part(): lax.all_gather(grad_out, 'local', axis=0, tiled=True)]
    all_gather x1 -> x0, waiting for transfers between devices: 75.6 us -> none  [shared_part(): lax.all_gather(tokens, 'local', axis=0, tiled=True)]
    all_to_all x1, starting transfers between devices: 11.2 us -> 35.4 us  [in_one_piece(): lax.all_to_all(both, axis, split_axis=split_dim, concat_axis=concat_dim,...]
    ppermute x0 -> x15, starting transfers between devices: none -> 22.1 us  [the longest x7 19.4 us: gather_around(): upper.append(lax.ppermute(upper[-1] if upper else x, axis, back))]
    all_to_all x1, starting transfers between devices: 8.77 us -> 26 us  [summed_on_arrival(): lax.all_to_all(tiles, axis, split_axis=0, concat_axis=0, tiled=True)]
    unnamed x32 -> x55, local copies, waits for them, and re-layouts: 11.2 us -> 28.3 us
    all_to_all x1, waiting for transfers between devices: 11.3 us -> 0.01 us  [in_one_piece(): lax.all_to_all(both, axis, split_axis=split_dim, concat_axis=concat_dim,...]
  transfers between devices with their start and end apart: 7 -> 21, of which waited for: 4 -> 10; matrix products, arithmetic and copies ran while one was open for 31% -> 31% of each run, Pallas kernels for 0% -> 0%
where the time goes in v1:
time: 591 us; the launch traced here: 583 us
  waiting for transfers between devices  270 us (46%)
  starting transfers between devices  105 us (18%)
  local copies, waits for them, and re-layouts  101 us (17%)
  matrix products  64.6 us (11%)
  other arithmetic  27.8 us (5%)
  between operations  14.7 us (2%)
    ppermute x7, waiting for transfers between devices, gather_around(): upper.append(lax.ppermute(upper[-1] if upper else x, axis, back))  178 us
    all_to_all x1, waiting for transfers between devices, routed_part(): lax.all_to_all(partial_value.reshape(got_in.shape), ('node', 'local'), sp...  70 us
    all_to_all x1, starting transfers between devices, in_one_piece(): lax.all_to_all(both, axis, split_axis=split_dim, concat_axis=concat_dim,...  35.4 us
    unnamed x55, local copies, waits for them, and re-layouts  28.3 us
    all_to_all x1, starting transfers between devices, summed_on_arrival(): lax.all_to_all(tiles, axis, split_axis=0, concat_axis=0, tiled=True)  26 us
    dot_general x4, matrix products, contract_last(): lax.dot_general(left, right, (((1,), (1,)), ((), ())), preferred_element_...  23.8 us
    ppermute x8, waiting for transfers between devices, gather_around(): lower.append(lax.ppermute(lower[-1] if lower else x, axis, pairs))  22.5 us
    ppermute x7, starting transfers between devices, gather_around(): upper.append(lax.ppermute(upper[-1] if upper else x, axis, back))  19.4 us
  transfers between devices with their start and end apart: 21, of which 10 were waited for; matrix products, arithmetic and copies ran while one was open for 31% of the time, Pallas kernels for 0%

profile of v1, /device:TPU:11, one launch (start us, length us, event | category | flops | bytes accessed | tf_op | source)
XLA Modules:
  0.0 583.2 jit_solution(12146316255756262873)
XLA Ops:
  8.5 5.5 collective-permute-done
  16.4 4.4 collective-permute-done.1
  20.9 3.3 collective-permute-start.9
  24.2 3.6 collective-permute-done.2
  28.6 3.3 collective-permute-start.10
  32.0 2.6 collective-permute-done.3
  36.7 3.6 collective-permute-start.11
  44.9 4.0 collective-permute-start.12
  48.9 2.9 collective-permute-done.5
  54.0 3.4 collective-permute-start.13
  57.4 1.9 collective-permute-done.6
  59.5 5.2 broadcast_in_dim.61
  64.7 5.2 broadcast_in_dim.63
  69.9 11.0 %pad_maximum_fusion = bf16[128,4,14337]{2,1,0:T(4,128)(2,1)} fusion(bf16[128,4,1]{2,1,0:T(4,128)(2,1)S(1)} %copy.67, bf16[128,4,7168]{2,1,0:T(4,128)(2,1)} %bitcast.129, bf16[128,4,7168]{2,1,0:T(4,128)(2,1)} %bitcast.128), kind=kLoop, calls=%fused_computation.1 | loop fusion | flops 44043264 | bytes 29362176 | tf_op jit(solution)/shard_map/concatenate | solution.py:45
  80.9 35.4 %all-to-all-start = ((bf16[128,4,14337]{2,1,0:T(4,128)(2,1)}), bf16[128,4,14337]{2,1,0:T(4,128)(2,1)}, u32[]{:S(2)}, u32[]{:S(2)}) async-start(bf16[128,4,14337]{2,1,0:T(4,128)(2,1)} %pad_maximum_fusion), calls=%async_computation | async-start | bytes 29622272 | tf_op jit(solution)/shard_map/all_to_all | solution.py:47
  117.0 1.6 bitcast_dynamic-update-slice_fusion.15
  118.6 1.6 bitcast_dynamic-update-slice_fusion.14
  121.9 1.7 bitcast_dynamic-update-slice_fusion.12
  123.6 1.6 bitcast_dynamic-update-slice_fusion.11
  132.5 1.6 bitcast_dynamic-update-slice_fusion.1
  134.1 176.9 %collective-permute-done.14 = bf16[16,7168]{1,0:T(8,128)(2,1)S(1)} collective-permute-done((bf16[16,7168]{1,0:T(8,128)(2,1)}, bf16[16,7168]{1,0:T(8,128)(2,1)S(1)}, u32[]{:S(2)}, u32[]{:S(2)}) %collective-permute-start.14) | collective-permute-done | bytes 229408 | tf_op jit(solution)/shard_map/ppermute | solution.py:25
  311.7 4.6 gather_fusion
  316.3 3.9 fusion.44
  321.8 3.9 multiply_convert_fusion.5
  329.1 3.0 pad_maximum_fusion.1
  332.2 8.3 %copy.90 = bf16[7168,384]{1,0:T(8,128)(2,1)} copy(bf16[7168,384]{0,1:T(8,128)(2,1)} %pad_maximum_fusion.1) | data formatting | bytes 11010048
  340.5 2.7 fusion.45
  343.2 2.9 fusion
  346.2 26.0 %all-to-all-start.2 = ((bf16[16,16,7168]{2,1,0:T(8,128)(2,1)}), bf16[16,16,7168]{2,1,0:T(8,128)(2,1)}, u32[]{:S(2)}, u32[]{:S(2)}) async-start(bf16[16,16,7168]{2,1,0:T(8,128)(2,1)} %bitcast.130), calls=%async_computation.2 | async-start | bytes 7340032 | tf_op jit(solution)/shard_map/all_to_all | solution.py:39
  372.2 15.2 %fusion.41 = (bf16[128,4,7168]{2,1,0:T(4,128)(2,1)}, bf16[128,4,7168]{2,1,0:T(4,128)(2,1)}) fusion(bf16[128,4,14337]{2,1,0:T(4,128)(2,1)} %all-to-all-done), kind=kLoop, calls=%fused_computation.90 | loop fusion | bytes 29360128 | tf_op jit(solution)/shard_map/slice | solution.py:52
  388.6 12.2 %reshape.144 = bf16[512,7168]{1,0:T(8,128)(2,1)} reshape(bf16[128,4,7168]{2,1,0:T(4,128)(2,1)} %get-tuple-element.48) | data formatting | bytes 14680064 | tf_op jit(solution)/shard_map/reshape | solution.py:178
  400.8 12.1 %reshape.145 = bf16[512,7168]{1,0:T(8,128)(2,1)} reshape(bf16[128,4,7168]{2,1,0:T(4,128)(2,1)} %get-tuple-element.49) | data formatting | bytes 14680064 | tf_op jit(solution)/shard_map/reshape | solution.py:177
  412.9 5.8 fusion.9
  418.7 2.5 fusion.12
  422.3 2.6 multiply_reduce_fusion
  425.7 7.3 %fusion.7 = f32[512,7168]{1,0:T(8,128)} fusion(bf16[512,128]{0,1:T(8,128)(2,1)S(1)} %get-tuple-element.51, bf16[1,7168,128]{2,1,0:T(8,128)(2,1)S(1)} %copy-done), kind=kOutput, calls=%fused_computation.23 | convolution fusion | flops 939524096 | bytes 16646144 | tf_op jit(solution)/shard_map/dot_general | solution.py:70
  433.0 10.7 %all-to-all-start.3 = ((bf16[128,1,4]{2,1,0:T(2,128)(2,1)}), bf16[128,1,4]{2,1,0:T(2,128)(2,1)S(1)}, u32[]{:S(2)}, u32[]{:S(2)}) async-start(bf16[128,1,4]{2,1,0:T(2,128)(2,1)} %convert_element_type.134), calls=%async_computation.3 | async-start | bytes 131072 | tf_op jit(solution)/shard_map/all_to_all | solution.py:192
  443.7 10.8 %add_convert_fusion = bf16[512,7168]{1,0:T(8,128)(2,1)} fusion(f32[512,7168]{1,0:T(8,128)} %fusion.7, bf16[512,128]{0,1:T(8,128)(2,1)S(1)} %get-tuple-element.55, bf16[1,7168,128]{2,1,0:T(8,128)(2,1)} %param.15), kind=kOutput, calls=%fused_computation.3 | convolution fusion | flops 946864128 | bytes 23986176 | tf_op jit(solution)/shard_map/dot_general | solution.py:70
  454.5 12.6 %reshape.146 = bf16[128,4,7168]{2,1,0:T(4,128)(2,1)} reshape(bf16[512,7168]{1,0:T(8,128)(2,1)} %add_convert_fusion) | data formatting | bytes 14680064 | tf_op jit(solution)/shard_map/reshape | solution.py:186
  467.1 10.3 %all-to-all-start.1 = ((bf16[128,4,7168]{2,1,0:T(4,128)(2,1)}), bf16[128,4,7168]{2,1,0:T(4,128)(2,1)}, u32[]{:S(2)}, u32[]{:S(2)}) async-start(bf16[128,4,7168]{2,1,0:T(4,128)(2,1)} %reshape.146), calls=%async_computation.1 | async-start | bytes 14680064 | tf_op jit(solution)/shard_map/all_to_all | solution.py:185
  477.5 2.7 convert_reduce_fusion.1
  480.2 6.6 %fusion.1 = bf16[1,7168,128]{2,1,0:T(8,128)(2,1)} fusion(bf16[512,7168]{1,0:T(8,128)(2,1)} %reshape.145, bf16[512,128]{0,1:T(8,128)(2,1)S(1)} %get-tuple-element.51), kind=kOutput, calls=%fused_computation.12 | convolution fusion | flops 940441600 | bytes 9306112 | tf_op jit(solution)/shard_map/dot_general | solution.py:64
  486.9 3.4 fusion.2
  490.2 3.4 fusion.3
  494.6 2.0 fusion.42
  496.6 70.0 %all-to-all-done.1 = bf16[128,4,7168]{2,1,0:T(4,128)(2,1)} async-done(((bf16[128,4,7168]{2,1,0:T(4,128)(2,1)}), bf16[128,4,7168]{2,1,0:T(4,128)(2,1)}, u32[]{:S(2)}, u32[]{:S(2)}) %all-to-all-start.1) | async-done | bytes 7340064 | tf_op jit(solution)/shard_map/all_to_all | solution.py:185
  566.6 6.8 %convert_reduce_fusion = f32[8,2,4,7168]{3,2,1,0:T(4,128)S(1)} fusion(bf16[128,4,7168]{2,1,0:T(4,128)(2,1)} %all-to-all-done.1), kind=kLoop, calls=%fused_computation.2 | loop fusion | flops 6881280 | bytes 9175040 | tf_op jit(solution)/shard_map/reduce_sum | solution.py:200
  573.4 2.7 fusion.6
  (108 shorter events, 32.8 us)
Async XLA Ops:
  7.2 405.7 %copy-start = (bf16[1,7168,128]{2,1,0:T(8,128)(2,1)S(1)}, bf16[1,7168,128]{2,1,0:T(8,128)(2,1)}, u32[]{:S(2)}) copy-start(bf16[1,7168,128]{2,1,0:T(8,128)(2,1)} %param.14) | copy-start | bytes 5505028
  7.2 314.6 %all-gather.2.cloned.1.call-start = ((), (), s32[]{:S(2)}) async-start(), calls=%async_computation.5 | async-start | bytes 3899392 | tf_op jit(solution)/shard_map/all_gather | solution.py:107
  7.2 6.8 %collective-permute-start = (bf16[16,7168]{1,0:T(8,128)(2,1)}, bf16[16,7168]{1,0:T(8,128)(2,1)S(1)}, u32[]{:S(2)}, u32[]{:S(2)}) collective-permute-start(bf16[16,7168]{1,0:T(8,128)(2,1)} %param.10), channel_id=1, source_target_pairs={{0,1},{1,2},{2,3},{3,4},{4,5},{5,6},{6,7},{7,8},{8,9},{9,10},{10,1... | collective-permute-start | bytes 688136 | tf_op jit(solution)/shard_map/ppermute | solution.py:23
  14.0 6.8 %collective-permute-start.1 = (bf16[16,7168]{1,0:T(8,128)(2,1)S(1)}, bf16[16,7168]{1,0:T(8,128)(2,1)S(1)}, u32[]{:S(2)}, u32[]{:S(2)}) collective-permute-start(bf16[16,7168]{1,0:T(8,128)(2,1)S(1)} %collective-permute-done), channel_id=1, source_target_pairs={{0,1},{1,2},{2,3},{3,4},{4,5},{5,6},{6,7},{7,8},{8,9},{9,10},{10,1... | collective-permute-start | bytes 688136 | tf_op jit(solution)/shard_map/ppermute | solution.py:23
  15.2 5.7 collective-permute-start.8
  20.8 7.0 %collective-permute-start.2 = (bf16[16,7168]{1,0:T(8,128)(2,1)S(1)}, bf16[16,7168]{1,0:T(8,128)(2,1)S(1)}, u32[]{:S(2)}, u32[]{:S(2)}) collective-permute-start(bf16[16,7168]{1,0:T(8,128)(2,1)S(1)} %collective-permute-done.1), channel_id=1, source_target_pairs={{0,1},{1,2},{2,3},{3,4},{4,5},{5,6},{6,7},{7,8},{8,9},{9,10},{10,1... | collective-permute-start | bytes 688136 | tf_op jit(solution)/shard_map/ppermute | solution.py:23
  20.9 7.7 %collective-permute-start.9 = (bf16[16,7168]{1,0:T(8,128)(2,1)S(1)}, bf16[16,7168]{1,0:T(8,128)(2,1)S(1)}, u32[]{:S(2)}, u32[]{:S(2)}) collective-permute-start(bf16[16,7168]{1,0:T(8,128)(2,1)S(1)} %collective-permute-done.8), channel_id=1, source_target_pairs={{1,0},{2,1},{3,2},{4,3},{5,4},{6,5},{7,6},{8,7},{9,8},{10,9},{11,1... | collective-permute-start | bytes 688136 | tf_op jit(solution)/shard_map/ppermute | solution.py:25
  27.8 6.8 %collective-permute-start.3 = (bf16[16,7168]{1,0:T(8,128)(2,1)S(1)}, bf16[16,7168]{1,0:T(8,128)(2,1)}, u32[]{:S(2)}, u32[]{:S(2)}) collective-permute-start(bf16[16,7168]{1,0:T(8,128)(2,1)S(1)} %collective-permute-done.2), channel_id=1, source_target_pairs={{0,1},{1,2},{2,3},{3,4},{4,5},{5,6},{6,7},{7,8},{8,9},{9,10},{10,1... | collective-permute-start | bytes 688136 | tf_op jit(solution)/shard_map/ppermute | solution.py:23
  28.6 8.1 %collective-permute-start.10 = (bf16[16,7168]{1,0:T(8,128)(2,1)S(1)}, bf16[16,7168]{1,0:T(8,128)(2,1)S(1)}, u32[]{:S(2)}, u32[]{:S(2)}) collective-permute-start(bf16[16,7168]{1,0:T(8,128)(2,1)S(1)} %collective-permute-done.9), channel_id=1, source_target_pairs={{1,0},{2,1},{3,2},{4,3},{5,4},{6,5},{7,6},{8,7},{9,8},{10,9},{11,1... | collective-permute-start | bytes 688136 | tf_op jit(solution)/shard_map/ppermute | solution.py:25
  34.6 7.3 %collective-permute-start.4 = (bf16[16,7168]{1,0:T(8,128)(2,1)}, bf16[16,7168]{1,0:T(8,128)(2,1)}, u32[]{:S(2)}, u32[]{:S(2)}) collective-permute-start(bf16[16,7168]{1,0:T(8,128)(2,1)} %collective-permute-done.3), channel_id=1, source_target_pairs={{0,1},{1,2},{2,3},{3,4},{4,5},{5,6},{6,7},{7,8},{8,9},{9,10},{10,1... | collective-permute-start | bytes 688136 | tf_op jit(solution)/shard_map/ppermute | solution.py:23
  36.7 8.1 %collective-permute-start.11 = (bf16[16,7168]{1,0:T(8,128)(2,1)S(1)}, bf16[16,7168]{1,0:T(8,128)(2,1)S(1)}, u32[]{:S(2)}, u32[]{:S(2)}) collective-permute-start(bf16[16,7168]{1,0:T(8,128)(2,1)S(1)} %collective-permute-done.10), channel_id=1, source_target_pairs={{1,0},{2,1},{3,2},{4,3},{5,4},{6,5},{7,6},{8,7},{9,8},{10,9},{11,1... | collective-permute-start | bytes 688136 | tf_op jit(solution)/shard_map/ppermute | solution.py:25
  41.9 9.9 %collective-permute-start.5 = (bf16[16,7168]{1,0:T(8,128)(2,1)}, bf16[16,7168]{1,0:T(8,128)(2,1)S(1)}, u32[]{:S(2)}, u32[]{:S(2)}) collective-permute-start(bf16[16,7168]{1,0:T(8,128)(2,1)} %collective-permute-done.4), channel_id=1, source_target_pairs={{0,1},{1,2},{2,3},{3,4},{4,5},{5,6},{6,7},{7,8},{8,9},{9,10},{10,1... | collective-permute-start | bytes 688136 | tf_op jit(solution)/shard_map/ppermute | solution.py:23
  44.9 19.8 %copy-start.11 = (bf16[16,7168]{1,0:T(8,128)(2,1)}, bf16[16,7168]{1,0:T(8,128)(2,1)S(1)}, u32[]{:S(2)}) copy-start(bf16[16,7168]{1,0:T(8,128)(2,1)S(1)} %collective-permute-done.11) | copy-start | bytes 688132
  44.9 9.1 %collective-permute-start.12 = (bf16[16,7168]{1,0:T(8,128)(2,1)S(1)}, bf16[16,7168]{1,0:T(8,128)(2,1)}, u32[]{:S(2)}, u32[]{:S(2)}) collective-permute-start(bf16[16,7168]{1,0:T(8,128)(2,1)S(1)} %collective-permute-done.11), channel_id=1, source_target_pairs={{1,0},{2,1},{3,2},{4,3},{5,4},{6,5},{7,6},{8,7},{9,8},{10,9},{11,1... | collective-permute-start | bytes 688136 | tf_op jit(solution)/shard_map/ppermute | solution.py:25
  51.8 12.9 %copy-start.13 = (bf16[16,7168]{1,0:T(8,128)(2,1)}, bf16[16,7168]{1,0:T(8,128)(2,1)S(1)}, u32[]{:S(2)}) copy-start(bf16[16,7168]{1,0:T(8,128)(2,1)S(1)} %collective-permute-done.5) | copy-start | bytes 688132
  51.8 7.5 %collective-permute-start.6 = (bf16[16,7168]{1,0:T(8,128)(2,1)S(1)}, bf16[16,7168]{1,0:T(8,128)(2,1)}, u32[]{:S(2)}, u32[]{:S(2)}) collective-permute-start(bf16[16,7168]{1,0:T(8,128)(2,1)S(1)} %collective-permute-done.5), channel_id=1, source_target_pairs={{0,1},{1,2},{2,3},{3,4},{4,5},{5,6},{6,7},{7,8},{8,9},{9,10},{10,1... | collective-permute-start | bytes 688136 | tf_op jit(solution)/shard_map/ppermute | solution.py:23
  54.0 62.4 %collective-permute-start.13 = (bf16[16,7168]{1,0:T(8,128)(2,1)}, bf16[16,7168]{1,0:T(8,128)(2,1)}, u32[]{:S(2)}, u32[]{:S(2)}) collective-permute-start(bf16[16,7168]{1,0:T(8,128)(2,1)} %collective-permute-done.12), channel_id=1, source_target_pairs={{1,0},{2,1},{3,2},{4,3},{5,4},{6,5},{7,6},{8,7},{9,8},{10,9},{11,1... | collective-permute-start | bytes 688136 | tf_op jit(solution)/shard_map/ppermute | solution.py:25
  59.3 57.7 %collective-permute-start.7 = (bf16[16,7168]{1,0:T(8,128)(2,1)}, bf16[16,7168]{1,0:T(8,128)(2,1)}, u32[]{:S(2)}, u32[]{:S(2)}) collective-permute-start(bf16[16,7168]{1,0:T(8,128)(2,1)} %collective-permute-done.6), channel_id=1, source_target_pairs={{0,1},{1,2},{2,3},{3,4},{4,5},{5,6},{6,7},{7,8},{8,9},{9,10},{10,1... | collective-permute-start | bytes 688136 | tf_op jit(solution)/shard_map/ppermute | solution.py:23
  80.9 265.3 %all-to-all-start = ((bf16[128,4,14337]{2,1,0:T(4,128)(2,1)}), bf16[128,4,14337]{2,1,0:T(4,128)(2,1)}, u32[]{:S(2)}, u32[]{:S(2)}) async-start(bf16[128,4,14337]{2,1,0:T(4,128)(2,1)} %pad_maximum_fusion), calls=%async_computation | async-start | bytes 29622272 | tf_op jit(solution)/shard_map/all_to_all | solution.py:47
  116.3 11.0 %copy-start.10 = (bf16[16,7168]{1,0:T(8,128)(2,1)S(1)}, bf16[16,7168]{1,0:T(8,128)(2,1)}, u32[]{:S(2)}) copy-start(bf16[16,7168]{1,0:T(8,128)(2,1)} %param.10) | copy-start | bytes 688132
  116.3 378.3 %reduce-scatter.4.cloned.1.call-start = ((), (), s32[]{:S(2)}) async-start(), calls=%async_computation.6 | async-start | bytes 6193152
  116.4 13.8 %copy-start.12 = (bf16[16,7168]{1,0:T(8,128)(2,1)S(1)}, bf16[16,7168]{1,0:T(8,128)(2,1)}, u32[]{:S(2)}) copy-start(bf16[16,7168]{1,0:T(8,128)(2,1)} %copy-done.11) | copy-start | bytes 688132
  116.4 194.6 %collective-permute-start.14 = (bf16[16,7168]{1,0:T(8,128)(2,1)}, bf16[16,7168]{1,0:T(8,128)(2,1)S(1)}, u32[]{:S(2)}, u32[]{:S(2)}) collective-permute-start(bf16[16,7168]{1,0:T(8,128)(2,1)} %collective-permute-done.13), channel_id=1, source_target_pairs={{1,0},{2,1},{3,2},{4,3},{5,4},{6,5},{7,6},{8,7},{9,8},{10,9},{11,1... | collective-permute-start | bytes 688136 | tf_op jit(solution)/shard_map/ppermute | solution.py:25
  316.3 3.9 copy-start.2
  316.3 4.3 copy-start.6
  321.8 3.9 copy-start.3
  326.4 2.0 copy-start.8
  340.5 2.8 copy-start.7
  346.2 86.8 %all-to-all-start.2 = ((bf16[16,16,7168]{2,1,0:T(8,128)(2,1)}), bf16[16,16,7168]{2,1,0:T(8,128)(2,1)}, u32[]{:S(2)}, u32[]{:S(2)}) async-start(bf16[16,16,7168]{2,1,0:T(8,128)(2,1)} %bitcast.130), calls=%async_computation.2 | async-start | bytes 7340032 | tf_op jit(solution)/shard_map/all_to_all | solution.py:39
  412.9 5.8 copy-start.1
  412.9 5.8 copy-start.5
  418.7 3.1 copy-start.4
  418.7 3.6 copy-start.9
  433.0 34.1 %all-to-all-start.3 = ((bf16[128,1,4]{2,1,0:T(2,128)(2,1)}), bf16[128,1,4]{2,1,0:T(2,128)(2,1)S(1)}, u32[]{:S(2)}, u32[]{:S(2)}) async-start(bf16[128,1,4]{2,1,0:T(2,128)(2,1)} %convert_element_type.134), calls=%async_computation.3 | async-start | bytes 131072 | tf_op jit(solution)/shard_map/all_to_all | solution.py:192
  467.1 99.5 %all-to-all-start.1 = ((bf16[128,4,7168]{2,1,0:T(4,128)(2,1)}), bf16[128,4,7168]{2,1,0:T(4,128)(2,1)}, u32[]{:S(2)}, u32[]{:S(2)}) async-start(bf16[128,4,7168]{2,1,0:T(4,128)(2,1)} %reshape.146), calls=%async_computation.1 | async-start | bytes 14680064 | tf_op jit(solution)/shard_map/all_to_all | solution.py:185
  477.5 9.4 %slice-start = ((s8[7340032]{0:T(1024)(128)(4,1)}), s8[4194304]{0:T(1024)(128)(4,1)S(1)}, s32[]{:S(2)}) async-start(s8[7340032]{0:T(1024)(128)(4,1)} %bitcast.120), calls=%async_computation.7 | async-start | bytes 8388608
  480.2 6.6 %slice-start.1 = ((s8[7340032]{0:T(1024)(128)(4,1)}), s8[3145728]{0:T(1024)(128)(4,1)S(1)}, s32[]{:S(2)}) async-start(s8[7340032]{0:T(1024)(128)(4,1)} %bitcast.120), calls=%async_computation.8 | async-start | bytes 6291456
  480.2 10.0 %slice-start.2 = ((s8[7340032]{0:T(1024)(128)(4,1)}), s8[4194304]{0:T(1024)(128)(4,1)S(1)}, s32[]{:S(2)}) async-start(s8[7340032]{0:T(1024)(128)(4,1)} %bitcast.126), calls=%async_computation.9 | async-start | bytes 8388608
  486.9 3.4 slice-start.3
  490.2 3.6 copy-start.14
Sparse Core Ops, SparseCore 0:
  21.0 65.7 all-gather.1
  340.6 59.4 reduce-scatter.3
